TPU v7x, 32 devices: a whole 2x2x4 slice. The times are simulated.
32 devices in a mesh: dp: 8 (over y, x, core), mp: 4 (over z).
Axes of the slice: x: 2, y: 2, z: 4, core: 2. Of those that a mesh axis runs over, the one named last changes fastest.
Arguments:
- tokens: bfloat16 [8192, 2048], P('dp'), may hold values from -6 to 6
- cotangent: bfloat16 [8192, 2048], P('dp'), may hold values from -6 to 6
- counts: int32 [8], replicated, may hold values from 1 to 1024, 5120 in all
- w_qkv: bfloat16 [2048, 3, 2048], P('dp', None, 'mp'), may hold values from -0.125 to 0.125
- w_out: bfloat16 [2048, 2048], P('mp', 'dp'), may hold values from -1 to 1
- w_fc1: bfloat16 [2048, 8192], P('dp', 'mp'), may hold values from -0.125 to 0.125
- w_fc2: bfloat16 [8192, 2048], P('mp', 'dp'), may hold values from -0.0625 to 0.0625
- ln1_gain: bfloat16 [2048], P('dp'), may hold values from 0.5 to 1.5
- ln1_bias: bfloat16 [2048], P('dp'), may hold values from -1.796875 to 1.796875
- ln2_gain: bfloat16 [2048], P('dp'), may hold values from 0.5 to 1.5
- ln2_bias: bfloat16 [2048], P('dp'), may hold values from -1.796875 to 1.796875
- qv_bias: bfloat16 [2, 2048], P(None, ('mp', 'dp')), may hold values from -1.796875 to 1.796875
- out_bias: bfloat16 [2048], P('dp'), may hold values from -1.796875 to 1.796875
- fc1_bias: bfloat16 [8192], P(('mp', 'dp')), may hold values from -1.796875 to 1.796875
- fc2_bias: bfloat16 [2048], P('dp'), may hold values from -1.796875 to 1.796875
Outputs:
- out_tokens: bfloat16 [8192, 2048], P('dp')
- grad_tokens: float32 [8192, 2048], P('dp')
- grad_w_qkv: float32 [2048, 3, 2048], P('dp', None, 'mp')
- grad_w_out: float32 [2048, 2048], P('mp', 'dp')
- grad_w_fc1: float32 [2048, 8192], P('dp', 'mp')
- grad_w_fc2: float32 [8192, 2048], P('mp', 'dp')
- grad_ln1_gain: float32 [2048], P('dp')
- grad_ln1_bias: float32 [2048], P('dp')
- grad_ln2_gain: float32 [2048], P('dp')
- grad_ln2_bias: float32 [2048], P('dp')
- grad_qv_bias: float32 [2, 2048], P(None, ('mp', 'dp'))
- grad_out_bias: float32 [2048], P('dp')
- grad_fc1_bias: float32 [8192], P(('mp', 'dp'))
- grad_fc2_bias: float32 [2048], P('dp')
Inputs may be any that keep to these rules, and one draw needn't show every extreme that they name: counts[g] is the number of live tokens of group g's sequence, at the start of its 1024 slots; the largest count equals 1024.
All inputs are finite; a program needn't handle non-finite values.
Results may differ from a plain program's by a relative error of at most 0.014.
Values may be sent and summed in bfloat16 or wider, within the bound.
A program may use at most 192 MiB of HBM per device.

v0:
```python
import math
import jax
import jax.numpy as jnp
from jax import lax
from jax.sharding import PartitionSpec as P

HEAD = 128
EPS = 1e-05
NEG = -1e30


def layer_norm(values, gain_vec, shift_vec):
    center = values - jnp.mean(values, axis=-1, keepdims=True)
    spread = jnp.mean(center * center, axis=-1, keepdims=True)
    return center * lax.rsqrt(spread + EPS) * gain_vec + shift_vec


def smooth_gate(values):
    return jax.nn.gelu(values, approximate=True)


def causal_scores(queries, key_heads, inv_root):
    row_count = queries.shape[0]
    raw_scores = (
        jnp.einsum("qhd,khd->hqk", queries, key_heads, preferred_element_type=jnp.float32)
        * inv_root
    )
    future = lax.broadcasted_iota(jnp.int32, (row_count, row_count), 1) > lax.broadcasted_iota(
        jnp.int32, (row_count, row_count), 0
    )
    return jnp.where(future[None], NEG, raw_scores)


def shards(
    tokens,
    cotangent,
    counts,
    w_qkv,
    w_out,
    w_fc1,
    w_fc2,
    ln1_gain,
    ln1_bias,
    ln2_gain,
    ln2_bias,
    qv_bias,
    out_bias,
    fc1_bias,
    fc2_bias,
):
    gathered = (
        lax.all_gather(w_qkv, "dp", axis=0, tiled=True),
        lax.all_gather(w_out, "dp", axis=1, tiled=True),
        lax.all_gather(w_fc1, "dp", axis=0, tiled=True),
        lax.all_gather(w_fc2, "dp", axis=1, tiled=True),
        lax.all_gather(ln1_gain, "dp", axis=0, tiled=True),
        lax.all_gather(ln1_bias, "dp", axis=0, tiled=True),
        lax.all_gather(ln2_gain, "dp", axis=0, tiled=True),
        lax.all_gather(ln2_bias, "dp", axis=0, tiled=True),
        lax.all_gather(qv_bias, "dp", axis=1, tiled=True),
        lax.all_gather(out_bias, "dp", axis=0, tiled=True),
        lax.all_gather(fc1_bias, "dp", axis=0, tiled=True),
        lax.all_gather(fc2_bias, "dp", axis=0, tiled=True),
    )
    whole_qkv, whole_out, whole_fc1, whole_fc2 = (
        gathered[0],
        gathered[1],
        gathered[2],
        gathered[3],
    )
    gain_one = gathered[4].astype(jnp.float32)
    shift_one = gathered[5].astype(jnp.float32)
    gain_two = gathered[6].astype(jnp.float32)
    shift_two = gathered[7].astype(jnp.float32)
    bias_qv = gathered[8].astype(jnp.float32)
    bias_out = gathered[9].astype(jnp.float32)
    bias_fc1 = gathered[10].astype(jnp.float32)
    bias_fc2 = gathered[11].astype(jnp.float32)
    seq_rows = tokens.shape[0]
    local_width = whole_qkv.shape[2]
    heads_here = local_width // HEAD
    inv_root = 1.0 / math.sqrt(HEAD)
    inputs = tokens.astype(jnp.float32)
    normed_one = layer_norm(inputs, gain_one, shift_one).astype(jnp.bfloat16)
    projected = jnp.einsum("sd,dce->sce", normed_one, whole_qkv, preferred_element_type=jnp.float32)
    queries = (
        (projected[:, 0] + bias_qv[0]).astype(jnp.bfloat16).reshape(seq_rows, heads_here, HEAD)
    )
    key_heads = projected[:, 1].astype(jnp.bfloat16).reshape(seq_rows, heads_here, HEAD)
    values = (projected[:, 2] + bias_qv[1]).astype(jnp.bfloat16).reshape(seq_rows, heads_here, HEAD)
    scores = causal_scores(queries, key_heads, inv_root)
    row_peak = jnp.max(scores, axis=-1, keepdims=True)
    exp_terms = jnp.exp(scores - row_peak)
    exp_total = jnp.sum(exp_terms, axis=-1, keepdims=True)
    log_total = row_peak + jnp.log(exp_total)
    prob_low = (exp_terms / exp_total).astype(jnp.bfloat16)
    mixed_heads = (
        jnp.einsum("hqk,khd->qhd", prob_low, values, preferred_element_type=jnp.float32)
        .astype(jnp.bfloat16)
        .reshape(seq_rows, local_width)
    )
    attn_part = jnp.dot(mixed_heads, whole_out, preferred_element_type=jnp.float32)
    residual = inputs + lax.psum(attn_part, "mp") + bias_out
    normed_two = layer_norm(residual, gain_two, shift_two).astype(jnp.bfloat16)
    preact = jnp.dot(normed_two, whole_fc1, preferred_element_type=jnp.float32) + bias_fc1
    activated = smooth_gate(preact).astype(jnp.bfloat16)
    ffn_part = jnp.dot(activated, whole_fc2, preferred_element_type=jnp.float32)
    out_tokens = (
        residual + lax.psum(ffn_part.astype(jnp.bfloat16), "mp").astype(jnp.float32) + bias_fc2
    ).astype(jnp.bfloat16)
    dp_index = lax.axis_index("dp")
    slot_ids = lax.iota(jnp.int32, counts.shape[0])
    own_count = jnp.sum(jnp.where(slot_ids == dp_index, counts, 0))
    weight_share = own_count.astype(jnp.float32) / jnp.sum(counts).astype(jnp.float32)
    live_rows = lax.iota(jnp.int32, seq_rows) < own_count
    grad_out = jnp.where(live_rows[:, None], cotangent.astype(jnp.float32), 0.0)
    grad_out_low = grad_out.astype(jnp.bfloat16)
    grad_fc2 = (
        jnp.einsum("sf,sd->fd", activated, grad_out_low, preferred_element_type=jnp.float32)
        * weight_share
    )
    grad_fc2_bias = jnp.sum(grad_out, axis=0) * weight_share
    delta_act = jnp.einsum("sd,fd->sf", grad_out_low, whole_fc2, preferred_element_type=jnp.float32)
    unused_gate, gate_back = jax.vjp(smooth_gate, preact)
    delta_pre = gate_back(delta_act)[0]
    grad_fc1_bias = jnp.sum(delta_pre, axis=0) * weight_share
    delta_pre_low = delta_pre.astype(jnp.bfloat16)
    grad_fc1 = (
        jnp.einsum("sd,sf->df", normed_two, delta_pre_low, preferred_element_type=jnp.float32)
        * weight_share
    )
    two_part = jnp.einsum("sf,df->sd", delta_pre_low, whole_fc1, preferred_element_type=jnp.float32)
    delta_two = lax.psum(two_part, "mp")
    unused_two, second_back = jax.vjp(layer_norm, residual, gain_two, shift_two)
    resid_part, gain_two_part, shift_two_part = second_back(delta_two)
    delta_resid = resid_part + grad_out
    delta_resid_low = delta_resid.astype(jnp.bfloat16)
    out_bias_part = jnp.sum(delta_resid, axis=0)
    grad_out_proj = (
        jnp.einsum("sc,sd->cd", mixed_heads, delta_resid_low, preferred_element_type=jnp.float32)
        * weight_share
    )
    delta_mixed = jnp.einsum(
        "sd,cd->sc", delta_resid_low, whole_out, preferred_element_type=jnp.float32
    )
    delta_mixed_low = delta_mixed.astype(jnp.bfloat16).reshape(seq_rows, heads_here, HEAD)
    scores_again = causal_scores(queries, key_heads, inv_root)
    prob_full = jnp.exp(scores_again - log_total)
    delta_prob = jnp.einsum(
        "qhd,khd->hqk", delta_mixed_low, values, preferred_element_type=jnp.float32
    )
    delta_scores = prob_full * (
        delta_prob - jnp.sum(prob_full * delta_prob, axis=-1, keepdims=True)
    )
    delta_scores_low = delta_scores.astype(jnp.bfloat16)
    delta_q = (
        jnp.einsum("hqk,khd->qhd", delta_scores_low, key_heads, preferred_element_type=jnp.float32)
        * inv_root
    ).reshape(seq_rows, local_width)
    delta_k = (
        jnp.einsum("hqk,qhd->khd", delta_scores_low, queries, preferred_element_type=jnp.float32)
        * inv_root
    ).reshape(seq_rows, local_width)
    delta_v = jnp.einsum(
        "hqk,qhd->khd", prob_low, delta_mixed_low, preferred_element_type=jnp.float32
    ).reshape(seq_rows, local_width)
    grad_qv = jnp.stack([jnp.sum(delta_q, axis=0), jnp.sum(delta_v, axis=0)]) * weight_share
    delta_proj = jnp.stack([delta_q, delta_k, delta_v], axis=1).astype(jnp.bfloat16)
    grad_qkv = (
        jnp.einsum("sd,sce->dce", normed_one, delta_proj, preferred_element_type=jnp.float32)
        * weight_share
    )
    one_part = jnp.einsum("sce,dce->sd", delta_proj, whole_qkv, preferred_element_type=jnp.float32)
    delta_one = lax.psum(one_part.astype(jnp.bfloat16), "mp").astype(jnp.float32)
    unused_one, first_back = jax.vjp(layer_norm, inputs, gain_one, shift_one)
    input_part, gain_one_part, shift_one_part = first_back(delta_one)
    grad_tokens = input_part + delta_resid
    stat_sums = jnp.stack(
        [gain_two_part, shift_two_part, out_bias_part, gain_one_part, shift_one_part]
    )
    stat_weighted = stat_sums * weight_share
    summed_all = (
        lax.psum_scatter(grad_qkv, "dp", scatter_dimension=0, tiled=True),
        lax.psum_scatter(grad_out_proj, "dp", scatter_dimension=1, tiled=True),
        lax.psum_scatter(grad_qv, "dp", scatter_dimension=1, tiled=True),
        lax.psum_scatter(stat_weighted[2], "dp", scatter_dimension=0, tiled=True),
        lax.psum_scatter(stat_weighted[3], "dp", scatter_dimension=0, tiled=True),
        lax.psum_scatter(stat_weighted[4], "dp", scatter_dimension=0, tiled=True),
        lax.psum_scatter(grad_fc1, "dp", scatter_dimension=0, tiled=True),
        lax.psum_scatter(grad_fc2, "dp", scatter_dimension=1, tiled=True),
        lax.psum_scatter(grad_fc1_bias, "dp", scatter_dimension=0, tiled=True),
        lax.psum_scatter(grad_fc2_bias, "dp", scatter_dimension=0, tiled=True),
        lax.psum_scatter(stat_weighted[0], "dp", scatter_dimension=0, tiled=True),
        lax.psum_scatter(stat_weighted[1], "dp", scatter_dimension=0, tiled=True),
    )
    return (
        out_tokens,
        grad_tokens,
        summed_all[0],
        summed_all[1],
        summed_all[6],
        summed_all[7],
        summed_all[4],
        summed_all[5],
        summed_all[10],
        summed_all[11],
        summed_all[2],
        summed_all[3],
        summed_all[8],
        summed_all[9],
    )


def solution(mesh):
    placed = (
        P("dp", None),
        P("dp", None),
        P(),
        P("dp", None, "mp"),
        P("mp", "dp"),
        P("dp", "mp"),
        P("mp", "dp"),
        P("dp"),
        P("dp"),
        P("dp"),
        P("dp"),
        P(None, ("mp", "dp")),
        P("dp"),
        P(("mp", "dp")),
        P("dp"),
    )
    return jax.shard_map(
        shards,
        mesh=mesh,
        in_specs=placed,
        out_specs=(
            P("dp", None),
            P("dp", None),
            P("dp", None, "mp"),
            P("mp", "dp"),
            P("dp", "mp"),
            P("mp", "dp"),
            P("dp"),
            P("dp"),
            P("dp"),
            P("dp"),
            P(None, ("mp", "dp")),
            P("dp"),
            P(("mp", "dp")),
            P("dp"),
        ),
        check_vma=False,
    )
```

profile of v0, /device:TPU:0, one launch (start us, length us, event | category | flops | bytes accessed | tf_op | source)
XLA Modules:
  0.0 1627.1 jit_solution(16595095688366546610)
XLA Ops:
  12.0 10.4 all-gather.2
  28.8 8.9 all-gather.1
  37.7 8.6 all-gather
  46.3 13.5 all-gather.13.cloned.1.call-done
  59.8 10.4 fusion.38
  79.8 8.1 fusion
  89.9 8.5 divide_convert_fusion
  112.2 9.1 all-gather.6
  129.3 8.9 all-gather.5
  147.5 254.6 %all-reduce.13.cloned.1.call-done = f32[1024,2048]{1,0:T(8,128)} async-done(((f32[1024,2048]{1,0:T(8,128)}), f32[1024,2048]{1,0:T(8,128)}) %all-reduce.13.cloned.1.call-update) | async-done | bytes 8388624 | tf_op jit(solution)/shard_map/psum | solution.py:103
  412.4 44.7 %all-gather.17.cloned.1.call-done = bf16[2048,2048]{1,0:T(8,128)(2,1)} async-done(((bf16[256,2048]{1,0:T(8,128)(2,1)}), bf16[2048,2048]{1,0:T(8,128)(2,1)}) %all-gather.17.cloned.1.call-update) | async-done | bytes 8388624 | tf_op jit(solution)/shard_map/all_gather | solution.py:54
  457.1 16.0 fusion.48
  473.1 41.7 %all-gather.19.cloned.1.call-done = bf16[2048,2048]{1,0:T(8,128)(2,1)} async-done(((bf16[2048,256]{1,0:T(8,128)(2,1)}), bf16[2048,2048]{1,0:T(8,128)(2,1)}) %all-gather.19.cloned.1.call-update) | async-done | bytes 8388624 | tf_op jit(solution)/shard_map/all_gather | solution.py:55
  514.7 20.5 %fusion.58 = (f32[2048]{0:T(1024)}, bf16[1024,2048]{1,0:T(8,128)(2,1)S(1)}) fusion(f32[1024,2048]{1,0:T(8,128)} %fusion.48, f32[2048]{0:T(1024)S(1)} %bitcast.123, bf16[2048,2048]{1,0:T(8,128)(2,1)} %all-gather.19.cloned.1.call-done, bf16[1024,2048]{1,0:T(8,128)(2,1)} %param.16, pred[1024]{0:T(1024)(128)(4,1)S(1)} %iota_compare_fusion.1), kind=kOutput, calls=%fused_computation.107 | convolution fusion | flops 8642361344 | bytes 25183232 | tf_op jit(solution)/shard_map/sd,fd->sf/dot_general | solution.py:123
  537.2 13.2 fusion.27
  551.9 16.9 %convolution_convert_fusion = bf16[1024,2048]{1,0:T(8,128)(2,1)} fusion(bf16[2048,2048]{1,0:T(8,128)(2,1)} %all-gather.19.cloned.1.call-done, f32[1024,2048]{1,0:T(8,128)} %fusion.48, f32[2048]{0:T(1024)S(1)} %bitcast.124), kind=kOutput, calls=%fused_computation.53 | convolution fusion | flops 8613003264 | bytes 20979712 | tf_op jit(solution)/shard_map/dot_general | solution.py:107
  568.8 272.7 %all-reduce.15.cloned.1.call-done = f32[1024,2048]{1,0:T(8,128)} async-done(((f32[1024,2048]{1,0:T(8,128)}), f32[1024,2048]{1,0:T(8,128)}) %all-reduce.15.cloned.1.call-update) | async-done | bytes 8388624 | tf_op jit(solution)/shard_map/psum | solution.py:133
  864.3 10.6 multiply_reduce_fusion
  874.9 12.4 multiply_convert_fusion
  902.1 11.0 bitcast_convert_fusion
  914.3 9.2 convolution_multiply_fusion.2
  923.6 17.6 %convolution_multiply_fusion = f32[2048,2048]{1,0:T(8,128)} fusion(f32[]{:T(128)S(6)} %div.63, bf16[1024,2048]{1,0:T(8,128)(2,1)} %param.16, pred[1024]{0:T(1024)(128)(4,1)S(1)} %iota_compare_fusion.1, f32[1024,2048]{1,0:T(8,128)} %fusion.48, f32[2048]{0:T(1024)S(1)} %bitcast.125), kind=kOutput, calls=%fused_computation.23 | convolution fusion | flops 8621391872 | bytes 29369348 | tf_op jit(solution)/shard_map/sf,sd->fd/dot_general | solution.py:119
  941.9 17.1 %convolution_multiply_fusion.1 = f32[2048,2048]{1,0:T(8,128)} fusion(f32[]{:T(128)S(6)} %div.63, bf16[1024,2048]{1,0:T(8,128)(2,1)} %copy-done.43, f32[1024,2048]{1,0:T(8,128)} %copy-done, f32[2048]{0:T(1024)S(1)} %bitcast.122, f32[2048]{0:T(1024)S(1)} %bitcast.98, f32[1024]{0:T(1024)S(1)} %fusion.42, f32[1024]{0:T(1024)S(1)} %broadcast_multiply_fusion.4), kind=kOutput, calls=%fused_computation.24 | convolution fusion | flops 8604614656 | bytes 29384708 | tf_op jit(solution)/shard_map/sd,sf->df/dot_general | solution.py:129
  960.3 13.7 broadcast_multiply_fusion
  974.6 8.9 all-gather.7
  986.2 242.6 %all-reduce.17.cloned.1.call-done = (bf16[1024,2048]{1,0:T(8,128)(2,1)}, bf16[1024,2048]{1,0:T(8,128)(2,1)}) async-done(((bf16[1024,2048]{1,0:T(8,128)(2,1)}, bf16[1024,2048]{1,0:T(8,128)(2,1)}), (bf16[1024,2048]{1,0:T(8,128)(2,1)}, bf16[1024,2048]{1,0:T(8,128)(2,1)})) %all-reduce.17.cloned.1.call-update) | async-done | bytes 8388624 | tf_op jit(solution)/shard_map/psum | solution.py:109
  1239.3 10.4 fusion.19
  1249.8 25.4 %all-reduce.7 = (f32[2048]{0:T(1024)S(1)}, f32[2048]{0:T(1024)S(1)}, f32[2048]{0:T(1024)S(1)}, f32[2048]{0:T(1024)S(1)}, f32[2048]{0:T(1024)S(1)}, /*index=5*/f32[2048]{0:T(1024)S(1)}, f32[2048]{0:T(1024)S(1)}) all-reduce(f32[2048]{0:T(1024)S(1)} %bitcast.111, f32[2048]{0:T(1024)S(1)} %bitcast.110, ...), channel_id=6, replica_groups=mesh['dp'=8,'mp'=4] {'dp'}, use_global_device_ids=true, to_apply=%region_26.27.clone | all-reduce | flops 14336 | bytes 114688
  1279.7 8.5 add_convert_fusion
  1288.2 115.5 %reduce-scatter.14.cloned.1.call-done = f32[2048,256]{1,0:T(8,128)} async-done(((f32[2048,2048]{1,0:T(8,128)}), f32[2048,256]{1,0:T(8,128)}) %reduce-scatter.14.cloned.1.call-update) | async-done | bytes 2097168 | tf_op jit(solution)/shard_map/reduce_scatter | solution.py:190
  1403.7 120.4 %reduce-scatter.12.cloned.1.call-done = f32[256,2048]{1,0:T(8,128)} async-done(((f32[2048,2048]{1,0:T(8,128)}), f32[256,2048]{1,0:T(8,128)}) %reduce-scatter.12.cloned.1.call-update) | async-done | bytes 2097168 | tf_op jit(solution)/shard_map/reduce_scatter | solution.py:189
  1524.0 96.0 %reduce-scatter.8.cloned.1.call-done = f32[256,3,512]{2,0,1:T(8,128)} async-done(((f32[2048,3,512]{2,0,1:T(8,128)}), f32[256,3,512]{2,0,1:T(8,128)}) %reduce-scatter.8.cloned.1.call-update) | async-done | bytes 1572880 | tf_op jit(solution)/shard_map/reduce_scatter | solution.py:183
  (191 shorter events, 124.1 us)
Async XLA Ops:
  7.2 52.6 %all-gather.13.cloned.1.call-start = ((), (), s32[]{:S(2)}) async-start(), calls=%async_computation.5 | async-start | bytes 7077888 | tf_op jit(solution)/shard_map/all_gather | solution.py:52
  9.5 93.5 %all-gather.15.cloned.1.call-start = ((), (), s32[]{:S(2)}) async-start(), calls=%async_computation.6 | async-start | bytes 2359296 | tf_op jit(solution)/shard_map/all_gather | solution.py:53
  10.3 391.8 %all-reduce.13.cloned.1.call-start = ((), (), s32[]{:S(2)}) async-start(), calls=%async_computation.7 | async-start | bytes 16777216 | tf_op jit(solution)/shard_map/psum | solution.py:103
  22.4 49.7 %copy-start.29 = (f32[1,512]{1,0:T(1,128)}, f32[1,512]{1,0:T(1,128)S(1)}, u32[]{:S(2)}) copy-start(f32[1,512]{1,0:T(1,128)S(1)} %get-tuple-element.47) | copy-start | bytes 6148
  25.3 44.9 %copy-start.21 = (f32[1024]{0:T(1024)}, f32[1024]{0:T(1024)S(1)}, u32[]{:S(2)}) copy-start(f32[1024]{0:T(1024)S(1)} %broadcast_multiply_fusion.5) | copy-start | bytes 12292
  28.8 8.9 copy-start.25
  28.8 41.5 %copy-start.23 = (f32[1024]{0:T(1024)}, f32[1024]{0:T(1024)S(1)}, u32[]{:S(2)}) copy-start(f32[1024]{0:T(1024)S(1)} %fusion.41) | copy-start | bytes 12292
  37.7 32.6 %copy-start.31 = (f32[8,1,256]{2,1,0:T(1,128)}, f32[8,1,256]{2,1,0:T(1,128)S(1)}, u32[]{:S(2)}) copy-start(f32[8,1,256]{2,1,0:T(1,128)S(1)} %convert_element_type.130) | copy-start | bytes 24580
  46.3 23.9 %copy-start.19 = (f32[8,1,256]{2,1,0:T(1,128)}, f32[8,1,256]{2,1,0:T(1,128)S(1)}, u32[]{:S(2)}) copy-start(f32[8,1,256]{2,1,0:T(1,128)S(1)} %convert_element_type.129) | copy-start | bytes 24580
  70.4 9.3 copy-start.10
  89.9 8.5 copy-start.8
  110.8 35.4 %copy-start.36 = (s32[8]{0:T(128)S(1)}, s32[8]{0:T(128)}, u32[]{:S(2)}) copy-start(s32[8]{0:T(128)} %param.17) | copy-start | bytes 100
  110.9 346.2 %all-gather.17.cloned.1.call-start = ((), (), s32[]{:S(2)}) async-start(), calls=%async_computation.8 | async-start | bytes 9437184 | tf_op jit(solution)/shard_map/all_gather | solution.py:54
  111.5 403.3 %all-gather.19.cloned.1.call-start = ((), (), s32[]{:S(2)}) async-start(), calls=%async_computation.9 | async-start | bytes 9437184 | tf_op jit(solution)/shard_map/all_gather | solution.py:55
  112.0 729.4 %all-reduce.15.cloned.1.call-start = ((), (), s32[]{:S(2)}) async-start(), calls=%async_computation.10 | async-start | bytes 16777216 | tf_op jit(solution)/shard_map/psum | solution.py:133
  138.2 318.9 %copy-start.34 = (f32[8,1,256]{2,1,0:T(1,128)}, f32[8,1,256]{2,1,0:T(1,128)S(1)}, u32[]{:S(2)}) copy-start(f32[8,1,256]{2,1,0:T(1,128)S(1)} %convert_element_type.134) | copy-start | bytes 24580
  550.5 434.4 %reduce-scatter.16.cloned.1.call-start = ((), (), s32[]{:S(2)}) async-start(), calls=%async_computation.15 | async-start | bytes 294912
  841.4 8.2 copy-start.5
  849.7 11.7 slice-start
  874.9 12.4 copy-start.7
  874.9 12.4 copy-start.30
  902.0 326.9 %all-reduce.17.cloned.1.call-start = ((), (), s32[]{:S(2)}) async-start(), calls=%async_computation.16 | async-start | bytes 16777216 | tf_op jit(solution)/shard_map/psum | solution.py:109
  913.1 375.1 %reduce-scatter.10.cloned.1.call-start = ((), (), s32[]{:S(2)}) async-start(), calls=%async_computation.12 | async-start | bytes 4718592 | tf_op jit(solution)/shard_map/reduce_scatter | solution.py:184
  923.5 480.1 %reduce-scatter.14.cloned.1.call-start = ((), (), s32[]{:S(2)}) async-start(), calls=%async_computation.14 | async-start | bytes 18874368 | tf_op jit(solution)/shard_map/reduce_scatter | solution.py:190
  941.2 582.8 %reduce-scatter.12.cloned.1.call-start = ((), (), s32[]{:S(2)}) async-start(), calls=%async_computation.13 | async-start | bytes 18874368 | tf_op jit(solution)/shard_map/reduce_scatter | solution.py:189
  959.0 661.0 %reduce-scatter.8.cloned.1.call-start = ((), (), s32[]{:S(2)}) async-start(), calls=%async_computation.11 | async-start | bytes 14155776 | tf_op jit(solution)/shard_map/reduce_scatter | solution.py:183
  974.0 9.6 copy-start.42
  974.0 10.8 copy-start.33
  974.0 260.5 %copy-start.26 = (f32[1024]{0:T(1024)S(1)}, f32[1024]{0:T(1024)}, u32[]{:S(2)}) copy-start(f32[1024]{0:T(1024)} %copy-done.25) | copy-start | bytes 12292
  1228.9 10.4 copy-start.13
  1239.2 10.4 copy-start.27
  1239.2 10.4 copy-start.28
  (26 other events, 84.7 us)
Sparse Core Ops, SparseCore 0:
  10.4 49.3 all-gather.12
  61.7 28.0 all-gather.14
  111.0 291.0 all-reduce.12
  403.8 53.2 all-gather.16
  458.8 55.8 all-gather.18
  550.6 290.8 all-reduce.14
  902.1 32.6 reduce-scatter.15
  938.0 290.8 all-reduce.16
  1232.8 50.8 reduce-scatter.9
  1287.7 115.9 reduce-scatter.13
  1407.8 116.1 reduce-scatter.11
  1527.9 92.0 reduce-scatter.7
where the time goes:
time: 1630 us
  waiting for transfers between devices  1200 us (74%)
  matrix products  190 us (12%)
  blocking collectives  96.2 us (6%)
  other arithmetic  87.9 us (5%)
  local copies, waits for them, and re-layouts  32.2 us (2%)
  between operations  17.2 us (1%)
    psum x1, waiting for transfers between devices, shards(): delta_two = lax.psum(two_part, 'mp')  273 us
    psum x1, waiting for transfers between devices, shards(): residual = inputs + lax.psum(attn_part, 'mp') + bias_out  255 us
    psum x1, waiting for transfers between devices, shards(): lax.psum(ffn_part.astype(jnp.bfloat16), 'mp').astype(jnp.float32)  243 us
    reduce_scatter x1, waiting for transfers between devices, shards(): lax.psum_scatter(grad_fc1, 'dp', scatter_dimension=0, tiled=True)  120 us
    reduce_scatter x1, waiting for transfers between devices, shards(): lax.psum_scatter(grad_fc2, 'dp', scatter_dimension=1, tiled=True)  115 us
    reduce_scatter x1, waiting for transfers between devices, shards(): lax.psum_scatter(grad_qkv, 'dp', scatter_dimension=0, tiled=True)  96 us
    all_gather x1, waiting for transfers between devices, shards(): lax.all_gather(w_fc1, 'dp', axis=0, tiled=True)  44.7 us
    all_gather x1, waiting for transfers between devices, shards(): lax.all_gather(w_fc2, 'dp', axis=1, tiled=True)  41.7 us
  transfers between devices with their start and end apart: 12, of which 9 were waited for; matrix products, arithmetic and copies ran while one was open for 12% of the time, Pallas kernels for 0%

commit v1 on v0

--- a/solution.py
+++ b/solution.py
@@ -130,7 +130,13 @@
         * weight_share
     )
     two_part = jnp.einsum("sf,df->sd", delta_pre_low, whole_fc1, preferred_element_type=jnp.float32)
-    delta_two = lax.psum(two_part, "mp")
+    devices = lax.axis_size("mp")
+    delta_two, far = (two_part, 1)
+    while far < devices:
+        delta_two = delta_two + lax.ppermute(
+            delta_two, "mp", [(i, i ^ far) for i in range(devices)]
+        )
+        far = 2 * far
     unused_two, second_back = jax.vjp(layer_norm, residual, gain_two, shift_two)
     resid_part, gain_two_part, shift_two_part = second_back(delta_two)
     delta_resid = resid_part + grad_out

time: 1630 us -> 1900 us (1.17)
  waiting for transfers between devices: 1200 us -> 1460 us
    ppermute x0 -> x2, waiting for transfers between devices: none -> 524 us  [shards(): lax.ppermute(delta_two, 'mp', [(i, i ^ far) for i in range(devices)])]
    psum x1 -> x0, waiting for transfers between devices: 273 us -> none  [shards(): delta_two = lax.psum(two_part, 'mp')]
  transfers between devices with their start and end apart: 12 -> 13, of which waited for: 9 -> 10; matrix products, arithmetic and copies ran while one was open for 12% -> 10% of each run, Pallas kernels for 0% -> 0%
where the time goes in v1:
time: 1900 us
  waiting for transfers between devices  1460 us (77%)
  matrix products  188 us (10%)
  other arithmetic  99 us (5%)
  blocking collectives  96.5 us (5%)
  local copies, waits for them, and re-layouts  35.1 us (2%)
    ppermute x2, waiting for transfers between devices, shards(): lax.ppermute(delta_two, 'mp', [(i, i ^ far) for i in range(devices)])  524 us
    psum x1, waiting for transfers between devices, shards(): residual = inputs + lax.psum(attn_part, 'mp') + bias_out  255 us
    psum x1, waiting for transfers between devices, shards(): lax.psum(ffn_part.astype(jnp.bfloat16), 'mp').astype(jnp.float32)  245 us
    reduce_scatter x1, waiting for transfers between devices, shards(): lax.psum_scatter(grad_fc2, 'dp', scatter_dimension=1, tiled=True)  120 us
    reduce_scatter x1, waiting for transfers between devices, shards(): lax.psum_scatter(grad_fc1, 'dp', scatter_dimension=0, tiled=True)  116 us
    reduce_scatter x1, waiting for transfers between devices, shards(): lax.psum_scatter(grad_qkv, 'dp', scatter_dimension=0, tiled=True)  96.2 us
    all_gather x1, waiting for transfers between devices, shards(): lax.all_gather(w_fc1, 'dp', axis=0, tiled=True)  44.7 us
    all_gather x1, waiting for transfers between devices, shards(): lax.all_gather(w_fc2, 'dp', axis=1, tiled=True)  41.6 us
  transfers between devices with their start and end apart: 13, of which 10 were waited for; matrix products, arithmetic and copies ran while one was open for 10% of the time, Pallas kernels for 0%

profile of v1, /device:TPU:0, one launch (start us, length us, event | category | flops | bytes accessed | tf_op | source)
XLA Modules:
  0.0 1895.7 jit_solution(18335797854649424697)
XLA Ops:
  11.3 10.4 all-gather.1
  22.4 9.2 all-gather
  38.5 8.6 all-gather.2
  47.2 12.6 all-gather.13.cloned.1.call-done
  59.8 10.4 fusion.38
  111.8 9.1 all-gather.3
  129.0 8.8 all-gather.4
  147.2 254.5 %all-reduce.12.cloned.1.call-done = f32[1024,2048]{1,0:T(8,128)} async-done(((f32[1024,2048]{1,0:T(8,128)}), f32[1024,2048]{1,0:T(8,128)}) %all-reduce.12.cloned.1.call-update) | async-done | bytes 8388624 | tf_op jit(solution)/shard_map/psum | solution.py:103
  412.0 44.7 %all-gather.17.cloned.1.call-done = bf16[2048,2048]{1,0:T(8,128)(2,1)} async-done(((bf16[256,2048]{1,0:T(8,128)(2,1)}), bf16[2048,2048]{1,0:T(8,128)(2,1)}) %all-gather.17.cloned.1.call-update) | async-done | bytes 8388624 | tf_op jit(solution)/shard_map/all_gather | solution.py:54
  456.8 16.0 fusion.48
  472.8 41.6 %all-gather.19.cloned.1.call-done = bf16[2048,2048]{1,0:T(8,128)(2,1)} async-done(((bf16[2048,256]{1,0:T(8,128)(2,1)}), bf16[2048,2048]{1,0:T(8,128)(2,1)}) %all-gather.19.cloned.1.call-update) | async-done | bytes 8388624 | tf_op jit(solution)/shard_map/all_gather | solution.py:55
  514.4 20.5 %fusion.58 = (f32[2048]{0:T(1024)}, bf16[1024,2048]{1,0:T(8,128)(2,1)S(1)}) fusion(f32[1024,2048]{1,0:T(8,128)} %fusion.48, f32[2048]{0:T(1024)S(1)} %bitcast.121, bf16[2048,2048]{1,0:T(8,128)(2,1)} %all-gather.19.cloned.1.call-done, bf16[1024,2048]{1,0:T(8,128)(2,1)} %param.16, pred[1024]{0:T(1024)(128)(4,1)S(1)} %iota_compare_fusion.1), kind=kOutput, calls=%fused_computation.107 | convolution fusion | flops 8642361344 | bytes 25183232 | tf_op jit(solution)/shard_map/sd,fd->sf/dot_general | solution.py:123
  534.9 12.8 fusion.27
  552.4 181.2 %collective-permute-done = f32[1024,2048]{1,0:T(8,128)} collective-permute-done((f32[1024,2048]{1,0:T(8,128)S(1)}, f32[1024,2048]{1,0:T(8,128)}, u32[]{:S(2)}, u32[]{:S(2)}) %collective-permute-start) | collective-permute-done | bytes 8388640 | tf_op jit(solution)/shard_map/ppermute | solution.py:136
  733.6 11.7 add.172
  749.1 16.1 convolution_convert_fusion
  765.2 342.8 %collective-permute-done.1 = f32[1024,2048]{1,0:T(8,128)} collective-permute-done((f32[1024,2048]{1,0:T(8,128)}, f32[1024,2048]{1,0:T(8,128)}, u32[]{:S(2)}, u32[]{:S(2)}) %collective-permute-start.1) | collective-permute-done | bytes 8388640 | tf_op jit(solution)/shard_map/ppermute | solution.py:136
  1131.3 10.6 multiply_reduce_fusion
  1141.9 12.1 multiply_convert_fusion
  1169.9 11.0 bitcast_convert_fusion
  1182.1 9.2 convolution_multiply_fusion.2
  1191.3 16.4 convolution_multiply_fusion.1
  1207.8 17.8 convolution_multiply_fusion
  1227.2 13.6 broadcast_multiply_fusion
  1241.4 8.9 all-gather.7
  1253.0 244.7 %all-reduce.14.cloned.1.call-done = (bf16[1024,2048]{1,0:T(8,128)(2,1)}, bf16[1024,2048]{1,0:T(8,128)(2,1)}) async-done(((bf16[1024,2048]{1,0:T(8,128)(2,1)}, bf16[1024,2048]{1,0:T(8,128)(2,1)}), (bf16[1024,2048]{1,0:T(8,128)(2,1)}, bf16[1024,2048]{1,0:T(8,128)(2,1)})) %all-reduce.14.cloned.1.call-update) | async-done | bytes 8388624 | tf_op jit(solution)/shard_map/psum | solution.py:109
  1508.1 10.4 fusion.19
  1518.6 25.5 %all-reduce.7 = (f32[2048]{0:T(1024)S(1)}, f32[2048]{0:T(1024)S(1)}, f32[2048]{0:T(1024)S(1)}, f32[2048]{0:T(1024)S(1)}, f32[2048]{0:T(1024)S(1)}, /*index=5*/f32[2048]{0:T(1024)S(1)}, f32[2048]{0:T(1024)S(1)}) all-reduce(f32[2048]{0:T(1024)S(1)} %bitcast.111, f32[2048]{0:T(1024)S(1)} %bitcast.110, ...), channel_id=6, replica_groups=mesh['dp'=8,'mp'=4] {'dp'}, use_global_device_ids=true, to_apply=%region_25.26.clone | all-reduce | flops 14336 | bytes 114688
  1548.5 8.5 add_convert_fusion
  1556.9 115.9 %reduce-scatter.12.cloned.1.call-done = f32[256,2048]{1,0:T(8,128)} async-done(((f32[2048,2048]{1,0:T(8,128)}), f32[256,2048]{1,0:T(8,128)}) %reduce-scatter.12.cloned.1.call-update) | async-done | bytes 2097168 | tf_op jit(solution)/shard_map/reduce_scatter | solution.py:195
  1672.8 120.0 %reduce-scatter.14.cloned.1.call-done = f32[2048,256]{1,0:T(8,128)} async-done(((f32[2048,2048]{1,0:T(8,128)}), f32[2048,256]{1,0:T(8,128)}) %reduce-scatter.14.cloned.1.call-update) | async-done | bytes 2097168 | tf_op jit(solution)/shard_map/reduce_scatter | solution.py:196
  1792.8 96.2 %reduce-scatter.8.cloned.1.call-done = f32[256,3,512]{2,0,1:T(8,128)} async-done(((f32[2048,3,512]{2,0,1:T(8,128)}), f32[256,3,512]{2,0,1:T(8,128)}) %reduce-scatter.8.cloned.1.call-update) | async-done | bytes 1572880 | tf_op jit(solution)/shard_map/reduce_scatter | solution.py:189
  (197 shorter events, 147.1 us)
Async XLA Ops:
  7.2 31.3 %copy-start.37 = (bf16[2,64]{1,0:T(2,128)(2,1)S(1)}, bf16[2,64]{1,0:T(2,128)(2,1)}, u32[]{:S(2)}) copy-start(bf16[2,64]{1,0:T(2,128)(2,1)} %param.26) | copy-start | bytes 772
  7.2 52.6 %all-gather.13.cloned.1.call-start = ((), (), s32[]{:S(2)}) async-start(), calls=%async_computation.5 | async-start | bytes 7077888 | tf_op jit(solution)/shard_map/all_gather | solution.py:52
  9.5 93.2 %all-gather.15.cloned.1.call-start = ((), (), s32[]{:S(2)}) async-start(), calls=%async_computation.6 | async-start | bytes 2359296 | tf_op jit(solution)/shard_map/all_gather | solution.py:53
  10.3 391.5 %all-reduce.12.cloned.1.call-start = ((), (), s32[]{:S(2)}) async-start(), calls=%async_computation.7 | async-start | bytes 16777216 | tf_op jit(solution)/shard_map/psum | solution.py:103
  21.7 48.6 %copy-start.32 = (f32[8,1,256]{2,1,0:T(1,128)}, f32[8,1,256]{2,1,0:T(1,128)S(1)}, u32[]{:S(2)}) copy-start(f32[8,1,256]{2,1,0:T(1,128)S(1)} %convert_element_type.130) | copy-start | bytes 24580
  31.6 38.7 %copy-start.20 = (f32[8,1,256]{2,1,0:T(1,128)}, f32[8,1,256]{2,1,0:T(1,128)S(1)}, u32[]{:S(2)}) copy-start(f32[8,1,256]{2,1,0:T(1,128)S(1)} %convert_element_type.129) | copy-start | bytes 24580
  34.5 35.9 %copy-start.22 = (f32[1024]{0:T(1024)}, f32[1024]{0:T(1024)S(1)}, u32[]{:S(2)}) copy-start(f32[1024]{0:T(1024)S(1)} %broadcast_multiply_fusion.5) | copy-start | bytes 12292
  38.5 31.8 %copy-start.24 = (f32[1024]{0:T(1024)}, f32[1024]{0:T(1024)S(1)}, u32[]{:S(2)}) copy-start(f32[1024]{0:T(1024)S(1)} %fusion.41) | copy-start | bytes 12292
  47.2 25.0 %copy-start.30 = (f32[1,512]{1,0:T(1,128)}, f32[1,512]{1,0:T(1,128)S(1)}, u32[]{:S(2)}) copy-start(f32[1,512]{1,0:T(1,128)S(1)} %get-tuple-element.48) | copy-start | bytes 6148
  110.5 10.4 copy-start.40
  110.5 18.4 copy-start.41
  110.5 27.3 %copy-start.42 = (bf16[256]{0:T(256)(128)(2,1)S(1)}, bf16[256]{0:T(256)(128)(2,1)}, u32[]{:S(2)}) copy-start(bf16[256]{0:T(256)(128)(2,1)} %param.28) | copy-start | bytes 1540
  110.5 35.4 %copy-start.38 = (s32[8]{0:T(128)S(1)}, s32[8]{0:T(128)}, u32[]{:S(2)}) copy-start(s32[8]{0:T(128)} %param.17) | copy-start | bytes 100
  110.6 346.2 %all-gather.17.cloned.1.call-start = ((), (), s32[]{:S(2)}) async-start(), calls=%async_computation.8 | async-start | bytes 9437184 | tf_op jit(solution)/shard_map/all_gather | solution.py:54
  111.2 403.2 %all-gather.19.cloned.1.call-start = ((), (), s32[]{:S(2)}) async-start(), calls=%async_computation.9 | async-start | bytes 9437184 | tf_op jit(solution)/shard_map/all_gather | solution.py:55
  111.7 1139.9 %reduce-scatter.16.cloned.1.call-start = ((), (), s32[]{:S(2)}) async-start(), calls=%async_computation.14 | async-start | bytes 294912
  129.0 327.8 %copy-start.35 = (f32[8,1,256]{2,1,0:T(1,128)}, f32[8,1,256]{2,1,0:T(1,128)S(1)}, u32[]{:S(2)}) copy-start(f32[8,1,256]{2,1,0:T(1,128)S(1)} %convert_element_type.134) | copy-start | bytes 24580
  534.9 12.8 copy-start.45
  550.9 182.7 %collective-permute-start = (f32[1024,2048]{1,0:T(8,128)S(1)}, f32[1024,2048]{1,0:T(8,128)}, u32[]{:S(2)}, u32[]{:S(2)}) collective-permute-start(f32[1024,2048]{1,0:T(8,128)S(1)} %fusion.27), channel_id=1, source_target_pairs={{0,1},{1,0},{2,3},{3,2},{4,5},{5,4},{6,7},{7,6},{8,9},{9,8},{10,11... | collective-permute-start | bytes 25165832 | tf_op jit(solution)/shard_map/ppermute | solution.py:136
  745.3 362.7 %collective-permute-start.1 = (f32[1024,2048]{1,0:T(8,128)}, f32[1024,2048]{1,0:T(8,128)}, u32[]{:S(2)}, u32[]{:S(2)}) collective-permute-start(f32[1024,2048]{1,0:T(8,128)} %add.172), channel_id=1, source_target_pairs={{0,2},{1,3},{2,0},{3,1},{4,6},{5,7},{6,4},{7,5},{8,10},{9,11},{10,... | collective-permute-start | bytes 25165832 | tf_op jit(solution)/shard_map/ppermute | solution.py:136
  749.1 359.0 %copy-start.5 = (f32[1024,2048]{1,0:T(8,128)S(1)}, f32[1024,2048]{1,0:T(8,128)}, u32[]{:S(2)}) copy-start(f32[1024,2048]{1,0:T(8,128)} %add.172) | copy-start | bytes 25165828
  1116.4 11.9 slice-start
  1141.9 12.1 copy-start.7
  1141.9 12.1 copy-start.31
  1169.8 327.8 %all-reduce.14.cloned.1.call-start = ((), (), s32[]{:S(2)}) async-start(), calls=%async_computation.15 | async-start | bytes 16777216 | tf_op jit(solution)/shard_map/psum | solution.py:109
  1180.9 10.5 copy-start.36
  1180.9 376.1 %reduce-scatter.10.cloned.1.call-start = ((), (), s32[]{:S(2)}) async-start(), calls=%async_computation.11 | async-start | bytes 4718592 | tf_op jit(solution)/shard_map/reduce_scatter | solution.py:190
  1191.3 481.5 %reduce-scatter.12.cloned.1.call-start = ((), (), s32[]{:S(2)}) async-start(), calls=%async_computation.12 | async-start | bytes 18874368 | tf_op jit(solution)/shard_map/reduce_scatter | solution.py:195
  1207.8 585.1 %reduce-scatter.14.cloned.1.call-start = ((), (), s32[]{:S(2)}) async-start(), calls=%async_computation.13 | async-start | bytes 18874368 | tf_op jit(solution)/shard_map/reduce_scatter | solution.py:196
  1225.7 663.3 %reduce-scatter.8.cloned.1.call-start = ((), (), s32[]{:S(2)}) async-start(), calls=%async_computation.10 | async-start | bytes 14155776 | tf_op jit(solution)/shard_map/reduce_scatter | solution.py:189
  1240.7 10.8 copy-start.34
  1240.7 262.5 %copy-start.27 = (f32[1024]{0:T(1024)S(1)}, f32[1024]{0:T(1024)}, u32[]{:S(2)}) copy-start(f32[1024]{0:T(1024)} %copy-done.26) | copy-start | bytes 12292
  (29 other events, 140.9 us)
Sparse Core Ops, SparseCore 0:
  10.4 49.3 all-gather.12
  61.7 28.0 all-gather.14
  110.7 291.0 all-reduce.11
  403.5 53.2 all-gather.16
  458.5 55.8 all-gather.18
  1169.9 33.6 reduce-scatter.15
  1206.8 290.8 all-reduce.13
  1501.6 50.8 reduce-scatter.9
  1556.6 116.1 reduce-scatter.11
  1676.8 115.9 reduce-scatter.13
  1796.9 92.0 reduce-scatter.7
